TPU v7x, 32 devices: a whole 2x2x4 slice. The times are simulated.
32 devices in a mesh: reg: 4 (over y, core), prod: 8 (over z, x).
Axes of the slice: x: 2, y: 2, z: 4, core: 2. Of those that a mesh axis runs over, the one named last changes fastest.
Arguments:
- bottom_series_predictions: float32 [128, 256, 128], P('reg', 'prod'), may hold values from -6 to 6
- group_item_predictions: float32 [32, 256, 128], P('reg', 'prod'), may hold values from -18 to 18
- area_class_predictions: float32 [128, 32, 128], P('reg', 'prod'), may hold values from -18 to 18
- group_class_predictions: float32 [32, 32, 128], P('reg'), may hold values from -48 to 48
- bottom_series_precision: float32 [128, 256], P('reg', 'prod'), may hold values from 0.5 to 5
- group_item_precision: float32 [32, 256], P('reg', 'prod'), may hold values from 0.02 to 0.5
- area_class_precision: float32 [128, 32], P('reg', 'prod'), may hold values from 0.02 to 0.5
- group_class_precision: float32 [32, 32], P('reg'), may hold values from 0.002 to 0.05
- group_area_partition: int32 [32, 128], replicated, may hold values from -1 to 127, as said below
- class_item_partition: int32 [32, 128], replicated, may hold values from -1 to 255, as said below
Outputs:
- solution_field: float32 [128, 256, 128], P('reg', 'prod')
- residual: float32 [128, 256, 128], P('reg', 'prod')
Inputs may be any that keep to these rules, and one draw needn't show every extreme that they name: `group_area_partition`: every region stands in exactly one row; each row holds its parent's regions in its first slots and -1 in the rest; a parent has 1 to 97 regions, and some parent has exactly 97. `class_item_partition`: every product stands in exactly one row; each row holds its category's products in its first slots and -1 in the rest; a category has 1 to 128 products, and some category has exactly 128.
All inputs are finite; a program needn't handle non-finite values.
Results may differ from a plain program's by a relative error of at most 0.00011.
Values sent between devices are 32-bit elements; how exact they have to be, the bound alone decides.
A program may use at most 64 MiB of HBM per device.

v0:
```python
import jax
import jax.numpy as jnp
from jax import lax
from jax.sharding import PartitionSpec as P

ITERATIONS = 2


def member_local(table, first, count):
    items = first + jnp.arange(count, dtype=jnp.int32)
    return jnp.any(table[:, :, None] == items[None, None, :], axis=1).astype(jnp.float32)


def on_device(
    bottom_series_predictions,
    group_item_predictions,
    area_class_predictions,
    group_class_predictions,
    bottom_series_precision,
    group_item_precision,
    area_class_precision,
    group_class_precision,
    group_area_partition,
    class_item_partition,
):
    high = lax.Precision.HIGHEST
    areas_overall, items_overall, horizon_length = bottom_series_predictions.shape
    area_index_table = member_local(
        group_area_partition, lax.axis_index("reg") * areas_overall, areas_overall
    )
    item_index_table = member_local(
        class_item_partition, lax.axis_index("prod") * items_overall, items_overall
    )
    parent_share = area_index_table.shape[0] // lax.axis_size("reg")

    def disaggregate_onto(upper, lower):
        block = area_index_table
        total = jnp.einsum(
            "pr,pqh->rqh", block, lax.all_gather(upper, "reg", axis=0, tiled=True), precision=high
        )
        block = item_index_table
        return total + jnp.einsum(
            "crh,cq->rqh", lax.all_gather(lower, "prod", axis=0, tiled=True), block, precision=high
        )

    def replicate_across(corner):
        return jnp.einsum("pch,cq->pqh", corner, item_index_table, precision=high)

    def operate(field):
        rows_local = jnp.einsum("pr,rqh->pqh", area_index_table, field, precision=high)
        row_share = lax.psum_scatter(rows_local, "reg", scatter_dimension=0, tiled=True)
        col_share = lax.psum_scatter(
            jnp.einsum("cq,rqh->crh", item_index_table, field, precision=high),
            "prod",
            scatter_dimension=0,
            tiled=True,
        )
        partial_corner = jnp.einsum("pqh,cq->pch", rows_local, item_index_table, precision=high)
        whole = lax.psum(partial_corner, ("reg", "prod"))
        corner_share = lax.dynamic_slice_in_dim(
            whole, lax.axis_index("reg") * parent_share, parent_share, 0
        )
        upper = group_item_precision[:, :, None] * row_share + replicate_across(
            group_class_precision[:, :, None] * corner_share
        )
        lower = jnp.transpose(area_class_precision)[:, :, None] * col_share
        return bottom_series_precision[:, :, None] * field + disaggregate_onto(upper, lower)

    major_axis_first = group_item_precision[:, :, None] * group_item_predictions + replicate_across(
        group_class_precision[:, :, None] * group_class_predictions
    )
    lower_leading = jnp.transpose(
        area_class_precision[:, :, None] * area_class_predictions, (1, 0, 2)
    )
    system_source_term = bottom_series_precision[
        :, :, None
    ] * bottom_series_predictions + disaggregate_onto(major_axis_first, lower_leading)

    def two_products(vector, image):
        return lax.psum((jnp.sum(vector * vector), jnp.sum(vector * image)), ("reg", "prod"))

    solution_field = jnp.zeros_like(system_source_term)
    residual = system_source_term
    image = operate(residual)
    norm_now, product = two_products(residual, image)
    alpha = norm_now / product
    direction, along = (residual, image)
    for step in range(ITERATIONS):
        solution_field = solution_field + alpha * direction
        residual = residual - alpha * along
        if step + 1 < ITERATIONS:
            image = operate(residual)
            norm_next, product = two_products(residual, image)
            ratio = norm_next / norm_now
            alpha = norm_next / (product - ratio * norm_next / alpha)
            direction = residual + ratio * direction
            along = image + ratio * along
            norm_now = norm_next
    return (solution_field, residual)


def solution(mesh):
    return jax.shard_map(
        on_device,
        mesh=mesh,
        in_specs=(
            P("reg", "prod", None),
            P("reg", "prod", None),
            P("reg", "prod", None),
            P("reg", None, None),
            P("reg", "prod"),
            P("reg", "prod"),
            P("reg", "prod"),
            P("reg", None),
            P(),
            P(),
        ),
        out_specs=(P("reg", "prod", None), P("reg", "prod", None)),
        check_vma=False,
    )
```

profile of v0, /device:TPU:12, one launch (start us, length us, event | category | flops | bytes accessed | tf_op | source)
XLA Modules:
  0.0 496.7 jit_solution(14481580540045878076)
XLA Ops:
  8.0 0.0 all-reduce.5.cloned.1.call-start
  8.1 0.6 copy-done.5
  8.7 0.1 copy.71
  8.8 0.6 copy-done.6
  9.4 0.7 compare_reduce_fusion
  10.1 1.3 fusion.5
  11.4 6.9 %all_gather.18 = f32[32,32,128]{2,1,0:T(8,128)S(1)} all-gather(f32[8,32,128]{2,1,0:T(8,128)S(1)} %fusion.5), channel_id=1, replica_groups=mesh['reg'=4,'prod'=8] {'reg'}, dimensions={0}, use_global_device_ids=true | all-gather | bytes 655360 | tf_op jit(solution)/shard_map/all_gather | solution.py:39
  18.4 0.1 fusion.24
  18.4 29.1 %all_gather.19 = f32[32,32,128]{2,1,0:T(8,128)S(1)} all-gather(f32[4,32,128]{2,1,0:T(8,128)S(1)} %fusion.24), channel_id=1, replica_groups=mesh['reg'=4,'prod'=8] {'prod'}, dimensions={0}, use_global_device_ids=true | all-gather | bytes 589824 | tf_op jit(solution)/shard_map/all_gather | solution.py:43
  47.5 0.7 fusion.16
  48.2 0.7 compare_reduce_fusion.1
  48.9 1.3 fusion.2
  50.2 0.4 fusion.41
  50.6 1.5 convolution_bitcast_fusion.1
  52.1 0.0 reduce-scatter.5.cloned.1.call-start
  52.1 1.1 copy.80
  53.3 0.0 reduce-scatter.5.cloned.1.call-update
  53.3 0.0 reduce-scatter.7.cloned.1.call-start
  53.3 0.7 fusion.13
  54.1 1.1 copy.86
  55.2 0.0 all-reduce.7.cloned.1.call-start
  55.2 129.7 %all-reduce.5.cloned.1.call-done = f32[32,32,128]{2,1,0:T(8,128)} async-done(((f32[32,32,128]{2,1,0:T(8,128)}), f32[32,32,128]{2,1,0:T(8,128)}) %all-reduce.5.cloned.1.call-update) | async-done | bytes 524304 | tf_op jit(solution)/shard_map/psum | solution.py:59
  184.9 1.3 fusion.4
  186.2 6.5 %all_gather.20 = f32[32,32,128]{2,1,0:T(8,128)S(1)} all-gather(f32[8,32,128]{2,1,0:T(8,128)S(1)} %fusion.4), channel_id=1, replica_groups=mesh['reg'=4,'prod'=8] {'reg'}, dimensions={0}, use_global_device_ids=true | all-gather | bytes 655360 | tf_op jit(solution)/shard_map/all_gather | solution.py:39
  192.7 0.9 broadcast_multiply_fusion.1
  193.6 28.7 %all_gather.21 = f32[32,32,128]{2,1,0:T(8,128)S(1)} all-gather(f32[4,32,128]{2,1,0:T(8,128)S(1)} %broadcast_multiply_fusion.1), channel_id=1, replica_groups=mesh['reg'=4,'prod'=8] {'prod'}, dimensions={0}, use_global_device_ids=true | all-gather | bytes 589824 | tf_op jit(solution)/shard_map/all_gather | solution.py:43
  222.3 0.7 fusion.11
  223.1 1.6 multiply_reduce_fusion.2
  224.7 43.1 %all-reduce.1 = (f32[]{:T(128)}, f32[]{:T(128)}) all-reduce(f32[]{:T(128)} %get-tuple-element.13, f32[]{:T(128)} %get-tuple-element.12), channel_id=1, replica_groups=mesh['reg'=4,'prod'=8] {'reg','prod'}, use_global_device_ids=true, to_apply=%region_3.0 | all-reduce | flops 2 | bytes 16 | tf_op jit(solution)/shard_map/psum | solution.py:80
  269.0 0.1 multiply_subtract_fusion.1
  269.1 0.4 fusion.39
  269.5 1.5 convolution_bitcast_fusion
  271.0 0.0 reduce-scatter.9.cloned.1.call-start
  271.1 1.1 copy.90
  272.2 0.2 reduce-scatter.11.cloned.1.call-start
  272.5 0.7 fusion.8
  273.2 1.1 copy.96
  274.3 125.1 %all-reduce.7.cloned.1.call-done = f32[32,32,128]{2,1,0:T(8,128)} async-done(((f32[32,32,128]{2,1,0:T(8,128)}), f32[32,32,128]{2,1,0:T(8,128)}) %all-reduce.7.cloned.1.call-update) | async-done | bytes 524304 | tf_op jit(solution)/shard_map/psum | solution.py:59
  399.4 1.3 fusion.3
  400.7 6.5 %all_gather.22 = f32[32,32,128]{2,1,0:T(8,128)S(1)} all-gather(f32[8,32,128]{2,1,0:T(8,128)S(1)} %fusion.3), channel_id=1, replica_groups=mesh['reg'=4,'prod'=8] {'reg'}, dimensions={0}, use_global_device_ids=true | all-gather | bytes 655360 | tf_op jit(solution)/shard_map/all_gather | solution.py:39
  407.2 0.9 broadcast_multiply_fusion
  408.1 28.8 %all_gather.23 = f32[32,32,128]{2,1,0:T(8,128)S(1)} all-gather(f32[4,32,128]{2,1,0:T(8,128)S(1)} %broadcast_multiply_fusion), channel_id=1, replica_groups=mesh['reg'=4,'prod'=8] {'prod'}, dimensions={0}, use_global_device_ids=true | all-gather | bytes 589824 | tf_op jit(solution)/shard_map/all_gather | solution.py:43
  436.9 0.7 fusion.6
  437.6 1.6 multiply_reduce_fusion
  439.2 42.9 %all-reduce = (f32[]{:T(128)}, f32[]{:T(128)}) all-reduce(f32[]{:T(128)} %get-tuple-element.11, f32[]{:T(128)} %get-tuple-element.10), channel_id=1, replica_groups=mesh['reg'=4,'prod'=8] {'reg','prod'}, use_global_device_ids=true, to_apply=%region_10.0 | all-reduce | flops 2 | bytes 16 | tf_op jit(solution)/shard_map/psum | solution.py:80
  486.6 0.2 multiply_subtract_fusion
  486.9 1.1 copy.101
  488.0 1.1 copy.100
  (25 shorter events, 0.1 us)
Async XLA Ops:
  8.0 0.7 copy-start.5
  8.0 176.9 %all-reduce.5.cloned.1.call-start = ((), (), s32[]{:S(2)}) async-start(), calls=%async_computation.5 | async-start | bytes 1048576 | tf_op jit(solution)/shard_map/psum | solution.py:59
  8.7 0.7 copy-start.6
  9.4 0.7 copy-start.2
  9.4 0.7 copy-start.3
  11.4 6.9 %copy-start.1 = (f32[32,4,128]{2,1,0:T(4,128)S(1)}, f32[32,4,128]{2,1,0:T(4,128)}, u32[]{:S(2)}) copy-start(f32[32,4,128]{2,1,0:T(4,128)} %param.12) | copy-start | bytes 196612
  11.4 6.9 %copy-start.4 = (f32[32,4]{0,1:T(4,128)S(1)}, f32[32,4]{0,1:T(4,128)}, u32[]{:S(2)}) copy-start(f32[32,4]{0,1:T(4,128)} %param.16) | copy-start | bytes 1540
  47.5 0.7 copy-start.7
  47.5 1.4 copy-start
  52.1 132.8 %reduce-scatter.5.cloned.1.call-start = ((), (), s32[]{:S(2)}) async-start(), calls=%async_computation.4 | async-start | bytes 655360 | tf_op jit(solution)/shard_map/reduce_scatter | solution.py:51
  53.3 139.4 %reduce-scatter.7.cloned.1.call-start = ((), (), s32[]{:S(2)}) async-start(), calls=%async_computation.6 | async-start | bytes 589824 | tf_op jit(solution)/shard_map/reduce_scatter | solution.py:52
  55.2 344.2 %all-reduce.7.cloned.1.call-start = ((), (), s32[]{:S(2)}) async-start(), calls=%async_computation.8 | async-start | bytes 1048576 | tf_op jit(solution)/shard_map/psum | solution.py:59
  271.0 128.4 %reduce-scatter.9.cloned.1.call-start = ((), (), s32[]{:S(2)}) async-start(), calls=%async_computation.7 | async-start | bytes 655360 | tf_op jit(solution)/shard_map/reduce_scatter | solution.py:51
  272.2 134.9 %reduce-scatter.11.cloned.1.call-start = ((), (), s32[]{:S(2)}) async-start(), calls=%async_computation.9 | async-start | bytes 589824 | tf_op jit(solution)/shard_map/reduce_scatter | solution.py:52
Sparse Core Ops, SparseCore 0:
  52.2 132.6 all-reduce.4
  271.2 128.1 all-reduce.6
Sparse Core Ops, SparseCore 1:
  55.1 24.1 reduce-scatter.4
  83.0 63.4 reduce-scatter.6
  274.0 19.7 reduce-scatter.8
  297.7 63.5 reduce-scatter.10
where the time goes:
time: 498 us; the launch traced here: 497 us
  waiting for transfers between devices  255 us (51%)
  blocking collectives  192 us (39%)
  between operations  21.7 us (4%)
  matrix products  15.5 us (3%)
  local copies, waits for them, and re-layouts  8.02 us (2%)
    psum x2, waiting for transfers between devices, operate(): whole = lax.psum(partial_corner, ('reg', 'prod'))  255 us
    all_gather x3, blocking collectives, disaggregate_onto(): lax.all_gather(lower, 'prod', axis=0, tiled=True)  86.6 us
    psum x2, blocking collectives, two_products(): lax.psum((jnp.sum(vector * vector), jnp.sum(vector * image)), ('reg', 'pr...  86 us
    all_gather x3, blocking collectives, disaggregate_onto(): lax.all_gather(upper, 'reg', axis=0, tiled=True)  19.9 us
  transfers between devices with their start and end apart: 6, of which 2 were waited for; matrix products, arithmetic and copies ran while one was open for 2% of the time, Pallas kernels for 0%

commit v1 on v0

--- a/solution.py
+++ b/solution.py
@@ -56,7 +56,7 @@
             tiled=True,
         )
         partial_corner = jnp.einsum("pqh,cq->pch", rows_local, item_index_table, precision=high)
-        whole = lax.psum(partial_corner, ("reg", "prod"))
+        whole = jnp.sum(lax.all_gather(partial_corner, axis_name=("reg", "prod")), axis=0)
         corner_share = lax.dynamic_slice_in_dim(
             whole, lax.axis_index("reg") * parent_share, parent_share, 0
         )

time: 498 us -> 502 us (level)
  other arithmetic: 3.64 us -> 21.5 us
  waiting for transfers between devices: 255 us -> 240 us
    psum x2 -> x0, waiting for transfers between devices: 255 us -> none  [operate(): whole = lax.psum(partial_corner, ('reg', 'prod'))]
    reduce_scatter x2, waiting for transfers between devices: 0.01 us -> 240 us  [operate(): lax.psum_scatter(jnp.einsum('cq,rqh->crh', item_index_table, field, preci...]
    reduce_sum x0 -> x2, other arithmetic: none -> 15.6 us  [operate(): jnp.sum(lax.all_gather(partial_corner, axis_name=('reg', 'prod')), axis=0)]
  transfers between devices with their start and end apart: 6 -> 6, of which waited for: 2 -> 2; matrix products, arithmetic and copies ran while one was open for 2% -> 5% of each run, Pallas kernels for 0% -> 0%
where the time goes in v1:
time: 502 us; the launch traced here: 501 us
  waiting for transfers between devices  240 us (48%)
  blocking collectives  194 us (39%)
  other arithmetic  21.5 us (4%)
  between operations  21.3 us (4%)
  matrix products  16.6 us (3%)
  local copies, waits for them, and re-layouts  7.41 us (1%)
    reduce_scatter x2, waiting for transfers between devices, operate(): lax.psum_scatter(jnp.einsum('cq,rqh->crh', item_index_table, field, preci...  240 us
    all_gather x3, blocking collectives, disaggregate_onto(): lax.all_gather(lower, 'prod', axis=0, tiled=True)  88.2 us
    psum x2, blocking collectives, two_products(): lax.psum((jnp.sum(vector * vector), jnp.sum(vector * image)), ('reg', 'pr...  85.9 us
    all_gather x3, blocking collectives, disaggregate_onto(): lax.all_gather(upper, 'reg', axis=0, tiled=True)  19.8 us
    reduce_sum x2, other arithmetic, operate(): jnp.sum(lax.all_gather(partial_corner, axis_name=('reg', 'prod')), axis=0)  15.6 us
  transfers between devices with their start and end apart: 6, of which 2 were waited for; matrix products, arithmetic and copies ran while one was open for 5% of the time, Pallas kernels for 0%

profile of v1, /device:TPU:12, one launch (start us, length us, event | category | flops | bytes accessed | tf_op | source)
XLA Modules:
  0.0 500.6 jit_solution(6900620538386263515)
XLA Ops:
  8.0 0.0 reduce-scatter.7.cloned.1.call-start
  8.1 0.8 copy.79
  8.9 1.4 compare_reduce_fusion
  10.3 1.3 fusion.5
  11.6 6.8 %all_gather.30 = f32[32,32,128]{2,1,0:T(8,128)S(1)} all-gather(f32[8,32,128]{2,1,0:T(8,128)S(1)} %fusion.5), channel_id=1, replica_groups=mesh['reg'=4,'prod'=8] {'reg'}, dimensions={0}, use_global_device_ids=true | all-gather | bytes 655360 | tf_op jit(solution)/shard_map/all_gather | solution.py:39
  18.4 0.9 fusion.24
  19.3 29.0 %all_gather.31 = f32[32,32,128]{2,1,0:T(8,128)S(1)} all-gather(f32[4,32,128]{2,1,0:T(8,128)S(1)} %fusion.24), channel_id=1, replica_groups=mesh['reg'=4,'prod'=8] {'prod'}, dimensions={0}, use_global_device_ids=true | all-gather | bytes 589824 | tf_op jit(solution)/shard_map/all_gather | solution.py:43
  48.3 0.7 fusion.16
  49.1 1.4 compare_reduce_fusion.1
  50.5 2.4 fusion.2
  52.8 0.7 fusion.13
  53.6 1.1 copy.94
  54.7 0.0 all-gather.5.cloned.1.call-start
  54.7 0.4 fusion.41
  55.1 1.5 convolution_bitcast_fusion.1
  56.7 0.0 reduce-scatter.5.cloned.1.call-start
  56.7 1.1 copy.88
  57.8 0.0 reduce-scatter.11.cloned.1.call-start
  57.9 122.0 %reduce-scatter.7.cloned.1.call-done = f32[4,32,128]{2,1,0:T(8,128)} async-done(((f32[32,32,128]{2,1,0:T(8,128)}), f32[4,32,128]{2,1,0:T(8,128)}) %reduce-scatter.7.cloned.1.call-update) | async-done | bytes 65552 | tf_op jit(solution)/shard_map/reduce_scatter | solution.py:52
  179.9 0.9 broadcast_multiply_fusion.1
  180.8 29.6 %all_gather.35 = f32[32,32,128]{2,1,0:T(8,128)S(1)} all-gather(f32[4,32,128]{2,1,0:T(8,128)S(1)} %broadcast_multiply_fusion.1), channel_id=1, replica_groups=mesh['reg'=4,'prod'=8] {'prod'}, dimensions={0}, use_global_device_ids=true | all-gather | bytes 589824 | tf_op jit(solution)/shard_map/all_gather | solution.py:43
  210.4 0.7 fusion.11
  211.1 0.0 all-gather.5.cloned.1.call-done
  211.1 7.8 %reduce_sum.55 = f32[32,32,128]{2,1,0:T(8,128)S(1)} reduce(f32[32,32,32,128]{3,2,1,0:T(8,128)} %bitcast.74, f32[]{:T(128)} %constant.6.clone.1), dimensions={0}, to_apply=%region_5.0 | reduce | flops 4063232 | bytes 17301508 | tf_op jit(solution)/shard_map/reduce_sum | solution.py:59
  219.0 1.2 fusion.4
  220.2 6.5 %all_gather.34 = f32[32,32,128]{2,1,0:T(8,128)S(1)} all-gather(f32[8,32,128]{2,1,0:T(8,128)S(1)} %fusion.4), channel_id=1, replica_groups=mesh['reg'=4,'prod'=8] {'reg'}, dimensions={0}, use_global_device_ids=true | all-gather | bytes 655360 | tf_op jit(solution)/shard_map/all_gather | solution.py:39
  226.7 1.6 multiply_reduce_fusion.2
  228.3 43.0 %all-reduce.1 = (f32[]{:T(128)}, f32[]{:T(128)}) all-reduce(f32[]{:T(128)} %get-tuple-element.13, f32[]{:T(128)} %get-tuple-element.12), channel_id=1, replica_groups=mesh['reg'=4,'prod'=8] {'reg','prod'}, use_global_device_ids=true, to_apply=%region_3.0 | all-reduce | flops 2 | bytes 16 | tf_op jit(solution)/shard_map/psum | solution.py:80
  272.6 0.1 multiply_subtract_fusion.1
  272.7 0.7 fusion.8
  273.4 1.1 copy.104
  274.5 0.0 all-gather.7.cloned.1.call-start
  274.6 0.4 fusion.39
  275.0 1.5 convolution_bitcast_fusion
  276.5 0.0 reduce-scatter.9.cloned.1.call-start
  276.5 1.1 copy.98
  277.7 117.6 %reduce-scatter.11.cloned.1.call-done = f32[4,32,128]{2,1,0:T(8,128)} async-done(((f32[32,32,128]{2,1,0:T(8,128)}), f32[4,32,128]{2,1,0:T(8,128)}) %reduce-scatter.11.cloned.1.call-update) | async-done | bytes 65552 | tf_op jit(solution)/shard_map/reduce_scatter | solution.py:52
  395.3 0.9 broadcast_multiply_fusion
  396.2 29.6 %all_gather.39 = f32[32,32,128]{2,1,0:T(8,128)S(1)} all-gather(f32[4,32,128]{2,1,0:T(8,128)S(1)} %broadcast_multiply_fusion), channel_id=1, replica_groups=mesh['reg'=4,'prod'=8] {'prod'}, dimensions={0}, use_global_device_ids=true | all-gather | bytes 589824 | tf_op jit(solution)/shard_map/all_gather | solution.py:43
  425.8 0.7 fusion.6
  426.6 7.8 %reduce_sum.58 = f32[32,32,128]{2,1,0:T(8,128)S(1)} reduce(f32[32,32,32,128]{3,2,1,0:T(8,128)} %bitcast.75, f32[]{:T(128)} %constant.6.clone.1), dimensions={0}, to_apply=%region_12.0 | reduce | flops 4063232 | bytes 17301508 | tf_op jit(solution)/shard_map/reduce_sum | solution.py:59
  434.4 1.2 fusion.3
  435.6 6.5 %all_gather.38 = f32[32,32,128]{2,1,0:T(8,128)S(1)} all-gather(f32[8,32,128]{2,1,0:T(8,128)S(1)} %fusion.3), channel_id=1, replica_groups=mesh['reg'=4,'prod'=8] {'reg'}, dimensions={0}, use_global_device_ids=true | all-gather | bytes 655360 | tf_op jit(solution)/shard_map/all_gather | solution.py:39
  442.1 1.6 multiply_reduce_fusion
  443.7 42.8 %all-reduce = (f32[]{:T(128)}, f32[]{:T(128)}) all-reduce(f32[]{:T(128)} %get-tuple-element.11, f32[]{:T(128)} %get-tuple-element.10), channel_id=1, replica_groups=mesh['reg'=4,'prod'=8] {'reg','prod'}, use_global_device_ids=true, to_apply=%region_10.0 | all-reduce | flops 2 | bytes 16 | tf_op jit(solution)/shard_map/psum | solution.py:80
  491.0 0.2 multiply_subtract_fusion
  491.3 1.1 copy.109
  492.4 1.1 copy.108
  (17 shorter events, 0.2 us)
Async XLA Ops:
  8.0 210.9 %copy-start = (f32[8,32]{1,0:T(8,128)S(1)}, f32[8,32]{1,0:T(8,128)}, u32[]{:S(2)}) copy-start(f32[8,32]{1,0:T(8,128)} %param.17) | copy-start | bytes 3076
  8.0 210.9 %copy-start.1 = (f32[8,32]{1,0:T(8,128)S(1)}, f32[8,32]{1,0:T(8,128)}, u32[]{:S(2)}) copy-start(f32[8,32]{1,0:T(8,128)} %param.15) | copy-start | bytes 3076
  8.0 171.9 %reduce-scatter.7.cloned.1.call-start = ((), (), s32[]{:S(2)}) async-start(), calls=%async_computation.5 | async-start | bytes 589824 | tf_op jit(solution)/shard_map/reduce_scatter | solution.py:52
  54.7 156.4 %all-gather.5.cloned.1.call-start = ((), (), s32[]{:S(2)}) async-start(), calls=%async_computation.8 | async-start | bytes 17301504 | tf_op jit(solution)/shard_map/all_gather | solution.py:59
  55.1 340.2 %copy-start.2 = (f32[32,4]{0,1:T(4,128)S(1)}, f32[32,4]{0,1:T(4,128)}, u32[]{:S(2)}) copy-start(f32[32,4]{0,1:T(4,128)} %param.16) | copy-start | bytes 1540
  56.7 162.3 %reduce-scatter.5.cloned.1.call-start = ((), (), s32[]{:S(2)}) async-start(), calls=%async_computation.4 | async-start | bytes 655360 | tf_op jit(solution)/shard_map/reduce_scatter | solution.py:51
  57.8 337.4 %reduce-scatter.11.cloned.1.call-start = ((), (), s32[]{:S(2)}) async-start(), calls=%async_computation.7 | async-start | bytes 589824 | tf_op jit(solution)/shard_map/reduce_scatter | solution.py:52
  274.5 152.0 %all-gather.7.cloned.1.call-start = ((), (), s32[]{:S(2)}) async-start(), calls=%async_computation.9 | async-start | bytes 17301504 | tf_op jit(solution)/shard_map/all_gather | solution.py:59
  276.5 157.9 %reduce-scatter.9.cloned.1.call-start = ((), (), s32[]{:S(2)}) async-start(), calls=%async_computation.6 | async-start | bytes 655360 | tf_op jit(solution)/shard_map/reduce_scatter | solution.py:51
Sparse Core Ops, SparseCore 0:
  54.8 125.0 reduce-scatter.6
  182.4 20.6 reduce-scatter.4
  274.6 120.5 reduce-scatter.10
  397.6 20.6 reduce-scatter.8
Sparse Core Ops, SparseCore 1:
  58.7 118.9 all-gather.4
  278.6 114.5 all-gather.6
